TPU v7x, 32 devices: a whole 2x2x4 slice. The times are simulated.
32 devices in a mesh: row: 8 (over z, x), col: 4 (over y, core).
Axes of the slice: x: 2, y: 2, z: 4, core: 2. Of those that a mesh axis runs over, the one named last changes fastest.
Arguments:
- trailing: float32 [16384, 8192], P('row', 'col'), may hold values from -6 to 6
- vectors: float32 [16384, 256], P(('row', 'col')), may hold values from -0.1875 to 0.1875
- tfactor: float32 [256, 256], replicated, may hold values from -0.375 to 0.375
Outputs:
- updated: float32 [16384, 8192], P('row', 'col')
All inputs are finite; a program needn't handle non-finite values.
Results may differ from a plain program's by a relative error of at most 0.0003.
Values sent between devices are 32-bit elements.
A program may use at most 128 MiB of HBM per device.

v0:
```python
import jax
import jax.numpy as jnp
from jax import lax
from jax.sharding import PartitionSpec as P


def shards(trailing, vectors, tfactor):
    high = lax.Precision.HIGHEST
    near_vectors = lax.all_gather(vectors, "col", axis=0, tiled=True)
    partial_value = jnp.dot(
        near_vectors.T, trailing, precision=high, preferred_element_type=jnp.float32
    )
    summed = lax.psum(partial_value, "row")
    scaled = jnp.dot(tfactor, summed, precision=high, preferred_element_type=jnp.float32)
    change = jnp.dot(near_vectors, scaled, precision=high, preferred_element_type=jnp.float32)
    return trailing - change


def solution(mesh):
    placed = (P("row", "col"), P(("row", "col"), None), P())
    return jax.shard_map(
        shards, mesh=mesh, in_specs=placed, out_specs=P("row", "col"), check_vma=False
    )
```

profile of v0, /device:TPU:0, one launch (start us, length us, event | category | flops | bytes accessed | tf_op | source)
XLA Modules:
  0.0 203.1 jit_solution(18051398769543396435)
XLA Ops:
  6.5 0.0 copy-start
  6.5 0.0 all-gather.2.cloned.1.call-start
  6.5 0.7 all-gather.2.cloned.1.call-update
  7.3 0.0 all-reduce.2.cloned.1.call-start
  7.3 26.8 %all-gather.2.cloned.1.call-done = f32[2048,256]{1,0:T(8,128)} async-done(((f32[512,256]{1,0:T(8,128)}), f32[2048,256]{1,0:T(8,128)}) %all-gather.2.cloned.1.call-update) | async-done | bytes 2097168 | tf_op jit(solution)/shard_map/all_gather | solution.py:9
  34.1 18.3 %fusion = f32[256,2048]{1,0:T(8,128)} fusion(f32[2048,256]{1,0:T(8,128)} %all-gather.2.cloned.1.call-done, f32[2048,2048]{1,0:T(8,128)} %param.3), kind=kOutput, calls=%fused_computation.1 | convolution fusion | flops 12884901888 | bytes 20971520 | tf_op jit(solution)/shard_map/dot_general | solution.py:10
  52.4 0.0 all-reduce.2.cloned.1.call-update
  52.5 17.6 %copy.4 = f32[2048,2048]{0,1:T(8,128)} copy(f32[2048,2048]{1,0:T(8,128)} %param.3) | data formatting | bytes 33554432 | tf_op args[0]
  70.1 0.0 copy-start.2
  70.1 84.9 %all-reduce.2.cloned.1.call-done = f32[256,2048]{1,0:T(8,128)} async-done(((f32[256,2048]{1,0:T(8,128)}), f32[256,2048]{1,0:T(8,128)}) %all-reduce.2.cloned.1.call-update) | async-done | bytes 2097168 | tf_op jit(solution)/shard_map/psum | solution.py:13
  155.0 0.0 copy-done
  155.0 5.2 %fusion.1 = f32[2048,256]{1,0:T(8,128)S(1)} fusion(f32[256,2048]{1,0:T(8,128)} %all-reduce.2.cloned.1.call-done, f32[256,256]{1,0:T(8,128)S(1)} %copy-done), kind=kOutput, calls=%fused_computation.2 | convolution fusion | flops 1610612736 | bytes 4456448 | tf_op jit(solution)/shard_map/dot_general | solution.py:14
  160.1 0.0 copy-done.2
  160.1 18.5 %bitcast_subtract_fusion = f32[2048,2048]{0,1:T(8,128)} fusion(f32[2048,2048]{0,1:T(8,128)} %copy.4, f32[2048,256]{1,0:T(8,128)S(1)} %fusion.1, f32[2048,256]{1,0:T(8,128)S(1)} %copy-done.2), kind=kOutput, calls=%fused_computation | convolution fusion | flops 12889096192 | bytes 37748736 | tf_op jit(solution)/shard_map/dot_general | solution.py:15
  178.7 0.0 copy-start.1
  178.7 17.6 %copy.5 = f32[2048,2048]{1,0:T(8,128)} copy(f32[2048,2048]{0,1:T(8,128)} %bitcast_subtract_fusion) | data formatting | bytes 33554432 | tf_op jit(solution)/shard_map/sub | solution.py:16
  196.3 0.0 copy-done.1
Async XLA Ops:
  6.5 148.4 %copy-start = (f32[256,256]{1,0:T(8,128)S(1)}, f32[256,256]{1,0:T(8,128)}, u32[]{:S(2)}) copy-start(f32[256,256]{1,0:T(8,128)} %param.5) | copy-start | bytes 786436
  6.5 27.6 %all-gather.2.cloned.1.call-start = ((), (), s32[]{:S(2)}) async-start(), calls=%async_computation | async-start | bytes 2621440 | tf_op jit(solution)/shard_map/all_gather | solution.py:9
  7.3 147.7 %all-reduce.2.cloned.1.call-start = ((), (), s32[]{:S(2)}) async-start(), calls=%async_computation.1 | async-start | bytes 4194304 | tf_op jit(solution)/shard_map/psum | solution.py:13
  70.1 90.1 %copy-start.2 = (f32[2048,256]{1,0:T(8,128)S(1)}, f32[2048,256]{1,0:T(8,128)}, u32[]{:S(2)}) copy-start(f32[2048,256]{1,0:T(8,128)} %all-gather.2.cloned.1.call-done) | copy-start | bytes 6291460
  178.7 17.6 %copy-start.1 = (f32[256,256]{1,0:T(8,128)S(1)}, f32[256,256]{1,0:T(8,128)}, u32[]{:S(2)}) copy-start(f32[256,256]{1,0:T(8,128)} %param.5) | copy-start | bytes 786436
Sparse Core Ops, SparseCore 0:
  8.9 25.2 all-gather.1
  52.6 102.3 all-reduce.1
where the time goes:
time: 204 us; the launch traced here: 203 us
  waiting for transfers between devices  112 us (55%)
  matrix products  42 us (21%)
  local copies, waits for them, and re-layouts  35.3 us (17%)
  between operations  13.4 us (7%)
    psum x1, waiting for transfers between devices, shards(): summed = lax.psum(partial_value, 'row')  84.9 us
    all_gather x1, waiting for transfers between devices, shards(): near_vectors = lax.all_gather(vectors, 'col', axis=0, tiled=True)  26.8 us
    dot_general x1, matrix products, shards(): jnp.dot(near_vectors, scaled, precision=high, preferred_element_type=jnp....  18.5 us
    dot_general x1, matrix products, shards(): jnp.dot(near_vectors.T, trailing, precision=high, preferred_element_type=...  18.3 us
    sub x1, local copies, waits for them, and re-layouts, shards(): return trailing - change  17.6 us
    unnamed x7, local copies, waits for them, and re-layouts  17.6 us
    dot_general x1, matrix products, shards(): jnp.dot(tfactor, summed, precision=high, preferred_element_type=jnp.float32)  5.17 us
  transfers between devices with their start and end apart: 2, of which 2 were waited for; matrix products, arithmetic and copies ran while one was open for 9% of the time, Pallas kernels for 0%

commit v1 on v0

v1 whole, which is shorter than its diff:
```python
import functools

import jax
import jax.numpy as jnp
from jax import lax
from jax.experimental import pallas as pl
from jax.experimental.pallas import tpu as pltpu
from jax.sharding import PartitionSpec as P

MESH = pl.DeviceIdType.MESH
F32, BF16 = jnp.float32, jnp.bfloat16
PIECES = 4
QUARTERS = 4


def split(x):
    high = x.astype(BF16)
    return high, (x - high.astype(F32)).astype(BF16)


def dot3(a_high, a_low, b_high, b_low):
    dot = functools.partial(jnp.dot, preferred_element_type=F32)
    return dot(a_high, b_high) + (dot(a_low, b_high) + dot(a_high, b_low))


def sum_kernel(
    ring, c_hbm, v_ref, t_ref, c_ref, near, scaled,
    acc, vt_high, vt_low, got, c_sem,
    sib_send, sib_recv, y_send, y_recv, f_send, f_recv, r_send, r_recv, g_send, g_recv,
):
    row, col = lax.axis_index("row"), lax.axis_index("col")
    core, y = lax.rem(col, 2), lax.div(col, 2)
    sibling = y * 2 + (1 - core)
    across = (1 - y) * 2 + core
    across_sibling = (1 - y) * 2 + (1 - core)
    half = ring // 2
    z, x = lax.div(row, 2), lax.rem(row, 2)
    at = jnp.where(x == 0, z, ring - 1 - z)

    def row_of(place):
        return jnp.where(place < half, 2 * place, 2 * (ring - 1 - place) + 1)

    def wrap(i):
        return lax.rem(i + 2 * ring, ring)

    hops = (row_of(wrap(at + 1)), row_of(wrap(at - 1)))
    own, depth = v_ref.shape
    width = c_ref.shape[2]

    def place_of(i):
        step = lax.div(i, 2) + 1
        return wrap(jnp.where(lax.rem(i, 2) == 0, at - step, at + step)) if not isinstance(i, int) else wrap(
            at - (i // 2 + 1) if i % 2 == 0 else at + (i // 2 + 1))

    def chunk_of(i):
        return jnp.where(i == ring - 1, at, place_of(i))

    def c_copy(chunk):
        return pltpu.make_async_copy(
            c_hbm.at[:, pl.ds(pl.multiple_of(chunk * width, width), width)], c_ref.at[chunk], c_sem.at[chunk]
        )

    def load(i, carry):
        c_copy(chunk_of(i)).start()
        return carry

    lax.fori_loop(0, ring, load, 0)

    barrier = pltpu.get_barrier_semaphore()
    friends = [(row, sibling), (row, across), (hops[0], col), (hops[1], col)]
    for friend in friends:
        pl.semaphore_signal(barrier, inc=1, device_id=friend, device_id_type=MESH)
    pl.semaphore_wait(barrier, len(friends))

    def remote(src, dst, send, recv, to):
        return pltpu.make_async_remote_copy(
            src_ref=src, dst_ref=dst, send_sem=send, recv_sem=recv, device_id=to, device_id_type=MESH
        )

    size = own // PIECES
    y_copies = []
    for q in range(PIECES):
        rows = pl.ds(q * size, size)
        copy = remote(v_ref.at[rows], near.at[col, rows], y_send.at[q], y_recv.at[q], (row, across))
        copy.start()
        y_copies.append(copy)
    sib = remote(v_ref, near.at[col], sib_send, sib_recv, (row, sibling))
    sib.start()

    def keep(block, first, count):
        rows = pl.ds(first, count)
        high, low = split(near[block, rows].T)
        vt_high[block, :, rows] = high
        vt_low[block, :, rows] = low

    near[col] = v_ref[...]
    keep(col, 0, own)

    def product(chunk, block, first, count):
        rows = pl.ds(pl.multiple_of(block * own + first, size), count)
        high, low = split(c_ref[chunk, rows])
        part = pl.ds(first, count)
        return dot3(vt_high[block, :, part], vt_low[block, :, part], high, low)

    sib.wait()
    keep(sibling, 0, own)

    def begin(i, carry):
        chunk = chunk_of(i)
        c_copy(chunk).wait()
        acc[chunk] = product(chunk, col, 0, own) + product(chunk, sibling, 0, own)
        return carry

    lax.fori_loop(0, ring, begin, 0)

    def arrive(q):
        rows = pl.ds(q * size, size)
        y_copies[q].wait()
        forward = remote(near.at[across, rows], near.at[across, rows], f_send.at[q], f_recv.at[q], (row, sibling))
        forward.start()
        keep(across, q * size, size)
        forward.wait()
        keep(across_sibling, q * size, size)

    def add(i, q):
        chunk = chunk_of(i)
        acc[chunk] += product(chunk, across, q * size, size) + product(chunk, across_sibling, q * size, size)

    for q in range(PIECES - 1):
        arrive(q)

        def more(i, carry):
            add(i, q)
            return carry

        lax.fori_loop(0, ring, more, 0)
    last = PIECES - 1
    arrive(last)
    part = depth // (2 * QUARTERS)

    def rows_of(way, q):
        return pl.ds((way * QUARTERS + q) * part, part)

    def sum_send(way, step, q, src):
        rows = rows_of(way, q)
        return remote(src.at[rows], got.at[step, rows], r_send.at[way, step, q], r_recv.at[way, step, q], (hops[way], col))

    def finish(i, carry):
        add(i, last)
        return carry

    lax.fori_loop(0, 2, finish, 0)
    for q in range(QUARTERS):
        for way in range(2):
            sum_send(way, 0, q, acc.at[chunk_of(way)]).start()
    lax.fori_loop(2, ring, finish, 0)

    steps = ring - 1

    def reduce(step, carry):
        for q in range(QUARTERS):
            for way in range(2):
                rows = rows_of(way, q)
                chunk = wrap(at - 2 - step) if way == 0 else wrap(at + 2 + step)
                sum_send(way, step, q, got.at[step]).wait_recv()
                got[step, rows] += acc[chunk, rows]

                @pl.when(step < steps - 1)
                def _():
                    sum_send(way, step + 1, q, got.at[step]).start()

        return carry

    lax.fori_loop(0, steps, reduce, 0)

    t_high, t_low = split(t_ref[...])
    high, low = split(got[steps - 1])
    scaled[at] = dot3(t_high, t_low, high, low)

    def gather_send(way, step, q, chunk):
        rows = rows_of(way, q)
        ref = scaled.at[chunk, rows]
        return remote(ref, ref, g_send.at[way, step, q], g_recv.at[way, step, q], (hops[way], col))

    for q in range(QUARTERS):
        for way in range(2):
            gather_send(way, 0, q, at).start()

    def gather(step, carry):
        for q in range(QUARTERS):
            for way in range(2):
                chunk = wrap(at - 1 - step) if way == 0 else wrap(at + 1 + step)
                gather_send(way, step, q, chunk).wait_recv()

                @pl.when(step < steps - 1)
                def _():
                    gather_send(way, step + 1, q, chunk).start()

        return carry

    lax.fori_loop(0, steps, gather, 0)

    def sent(step, carry):
        for q in range(QUARTERS):
            for way in range(2):
                sum_send(way, step, q, got.at[step]).wait_send()
                gather_send(way, step, q, at).wait_send()
        return carry

    lax.fori_loop(0, steps, sent, 0)


def update_kernel(c_ref, near, scaled, out_hbm, v_high, v_low, stage, sem):
    ring, height, width = c_ref.shape
    blocks, own, _ = near.shape
    for b in range(blocks):
        v_high[pl.ds(b * own, own)], v_low[pl.ds(b * own, own)] = split(near[b])
    slots = stage.shape[0]

    def out_copy(chunk, slot):
        return pltpu.make_async_copy(
            stage.at[slot], out_hbm.at[:, pl.ds(pl.multiple_of(chunk * width, width), width)], sem.at[slot]
        )

    def step(chunk, carry):
        slot = lax.rem(chunk, slots)

        @pl.when(chunk >= slots)
        def _():
            out_copy(chunk - slots, slot).wait()

        high, low = split(scaled[chunk])
        for b in range(blocks):
            rows = pl.ds(b * own, own)
            stage[slot, rows] = c_ref[chunk, rows] - dot3(v_high[rows], v_low[rows], high, low)
        out_copy(chunk, slot).start()
        return carry

    lax.fori_loop(0, ring, step, 0)
    for i in range(slots):
        chunk = ring - slots + i
        out_copy(chunk, chunk % slots).wait()


def ring_shards(ring, trailing, vectors, tfactor):
    height, columns = trailing.shape
    own, depth = vectors.shape
    width = columns // ring
    blocks = height // own
    steps = ring - 1
    dma = pltpu.SemaphoreType.DMA
    vmem = pl.BlockSpec(memory_space=pltpu.VMEM)
    hbm = pl.BlockSpec(memory_space=pl.ANY)
    held, near, scaled = pl.pallas_call(
        functools.partial(sum_kernel, ring),
        out_shape=(
            pltpu.VMEM((ring, height, width), F32),
            pltpu.VMEM((blocks, own, depth), F32),
            pltpu.VMEM((ring, depth, width), F32),
        ),
        in_specs=[hbm, vmem, vmem],
        out_specs=(vmem, vmem, vmem),
        scratch_shapes=[
            pltpu.VMEM((ring, depth, width), F32),
            pltpu.VMEM((blocks, depth, own), BF16),
            pltpu.VMEM((blocks, depth, own), BF16),
            pltpu.VMEM((steps, depth, width), F32),
            dma((ring,)),
            dma, dma,
            dma((PIECES,)), dma((PIECES,)), dma((PIECES,)), dma((PIECES,)),
            dma((2, steps, QUARTERS)), dma((2, steps, QUARTERS)),
            dma((2, steps, QUARTERS)), dma((2, steps, QUARTERS)),
        ],
        compiler_params=pltpu.CompilerParams(
            collective_id=0, has_side_effects=True, vmem_limit_bytes=20 << 20
        ),
    )(trailing, vectors, tfactor)
    slots = min(4, ring)
    return pl.pallas_call(
        update_kernel,
        out_shape=jax.ShapeDtypeStruct((height, columns), F32),
        in_specs=[vmem, vmem, vmem],
        out_specs=hbm,
        scratch_shapes=[
            pltpu.VMEM((height, depth), BF16),
            pltpu.VMEM((height, depth), BF16),
            pltpu.VMEM((slots, height, width), F32),
            dma((slots,)),
        ],
        compiler_params=pltpu.CompilerParams(vmem_limit_bytes=20 << 20),
    )(held, near, scaled)


def plain_shards(trailing, vectors, tfactor):
    dot = functools.partial(jnp.dot, precision=lax.Precision.HIGH, preferred_element_type=F32)
    near_vectors = lax.all_gather(vectors, "col", axis=0, tiled=True)
    summed = lax.psum(dot(near_vectors.T, trailing), "row")
    return trailing - dot(near_vectors, dot(tfactor, summed))


def solution(mesh):
    ring, columns = mesh.shape["row"], mesh.shape["col"]
    placed = (P("row", "col"), P(("row", "col"), None), P())

    def shards(trailing, vectors, tfactor):
        width = trailing.shape[1] // ring
        if columns == 4 and ring % 2 == 0 and ring > 2 and width % 128 == 0:
            return ring_shards(ring, trailing, vectors, tfactor)
        return plain_shards(trailing, vectors, tfactor)

    return jax.shard_map(
        shards, mesh=mesh, in_specs=placed, out_specs=P("row", "col"), check_vma=False
    )
```

time: 204 us -> 88.6 us (0.43)
  waiting for transfers between devices: 112 us -> 0 us
  Pallas kernels: 0 us -> 86.4 us
  matrix products: 42 us -> 0 us
  local copies, waits for them, and re-layouts: 35.3 us -> 1.99 us
  between operations: 13.4 us -> 0.01 us
    pallas_call x0 -> x2, Pallas kernels: none -> 86.4 us  [the longest x1 76.8 us: ring_shards(): pl.pallas_call(functools.partial(sum_kernel, ring), out_shape=(pltpu.VMEM...]
    psum x1 -> x0, waiting for transfers between devices: 84.9 us -> none  [shards(): summed = lax.psum(partial_value, 'row')]
    dot_general x3 -> x0, matrix products: 42 us -> none  [the longest x1 18.5 us: shards(): jnp.dot(near_vectors, scaled, precision=high, preferred_element_type=jnp....]
    all_gather x1 -> x0, waiting for transfers between devices: 26.8 us -> none  [shards(): near_vectors = lax.all_gather(vectors, 'col', axis=0, tiled=True)]
    sub x1 -> x0, local copies, waits for them, and re-layouts: 17.6 us -> none  [shards(): return trailing - change]
    unnamed x7 -> x4, local copies, waits for them, and re-layouts: 17.6 us -> 1.99 us
  transfers between devices with their start and end apart: 2 -> 0, of which waited for: 2 -> 0; matrix products, arithmetic and copies ran while one was open for 9% -> 0% of each run, Pallas kernels for 0% -> 0%
where the time goes in v1:
time: 88.6 us; the launch traced here: 88.4 us
  Pallas kernels  86.4 us (98%)
  local copies, waits for them, and re-layouts  1.99 us (2%)
    pallas_call x1, Pallas kernels, ring_shards(): pl.pallas_call(functools.partial(sum_kernel, ring), out_shape=(pltpu.VMEM...  76.8 us
    pallas_call x1, Pallas kernels, ring_shards(): pl.pallas_call(update_kernel, out_shape=jax.ShapeDtypeStruct((height, col...  9.62 us
    unnamed x4, local copies, waits for them, and re-layouts  1.99 us

profile of v1, /device:TPU:0, one launch (start us, length us, event | category | flops | bytes accessed | tf_op | source)
XLA Modules:
  0.0 88.4 jit_solution(2192309791360873994)
XLA Ops:
  0.0 0.0 copy-start
  0.0 1.0 %copy-done = f32[512,256]{1,0:T(8,128)S(1)} copy-done((f32[512,256]{1,0:T(8,128)S(1)}, f32[512,256]{1,0:T(8,128)}, u32[]{:S(2)}) %copy-start) | copy-done | bytes 524312
  1.0 0.0 copy-start.1
  1.0 0.9 %copy-done.1 = f32[256,256]{1,0:T(8,128)S(1)} copy-done((f32[256,256]{1,0:T(8,128)S(1)}, f32[256,256]{1,0:T(8,128)}, u32[]{:S(2)}) %copy-start.1) | copy-done | bytes 262168
  2.0 76.8 %shard_map.37 = (f32[8,2048,256]{2,1,0:T(8,128)S(1)}, f32[4,512,256]{2,1,0:T(8,128)S(1)}, f32[8,256,256]{2,1,0:T(8,128)S(1)}) custom-call(f32[2048,2048]{1,0:T(8,128)} %c_hbm.1, f32[512,256]{1,0:T(8,128)S(1)} %copy-done, f32[256,256]{1,0:T(8,128)S(1)} %copy-done.1), custom_call_target="tpu_custom_call" | custom-call | tf_op jit(solution)/shard_map/pallas_call | solution.py:254
  78.8 9.6 %shard_map.38 = f32[2048,2048]{1,0:T(8,128)} custom-call(f32[8,2048,256]{2,1,0:T(8,128)S(1)} %get-tuple-element.8.c_ref, f32[4,512,256]{2,1,0:T(8,128)S(1)} %get-tuple-element.9.near, f32[8,256,256]{2,1,0:T(8,128)S(1)} %get-tuple-element.10.scaled), custom_call_target="tpu_custom_call" | custom-call | tf_op jit(solution)/shard_map/pallas_call | solution.py:279
Async XLA Ops:
  0.0 1.0 %copy-start = (f32[512,256]{1,0:T(8,128)S(1)}, f32[512,256]{1,0:T(8,128)}, u32[]{:S(2)}) copy-start(f32[512,256]{1,0:T(8,128)} %v_ref.1) | copy-start | bytes 1572868
  1.0 0.9 %copy-start.1 = (f32[256,256]{1,0:T(8,128)S(1)}, f32[256,256]{1,0:T(8,128)}, u32[]{:S(2)}) copy-start(f32[256,256]{1,0:T(8,128)} %t_ref.1) | copy-start | bytes 786436

commit v2 on v1

v2 whole, which is shorter than its diff:
```python
import functools

import jax
import jax.numpy as jnp
from jax import lax
from jax.experimental import pallas as pl
from jax.experimental.pallas import tpu as pltpu
from jax.sharding import PartitionSpec as P

MESH = pl.DeviceIdType.MESH
F32, BF16 = jnp.float32, jnp.bfloat16
HALVES = 2
PIECES = 2
QUARTERS = 2
G_QUARTERS = 4
LAG = 3


def split(x):
    high = x.astype(BF16)
    return high, (x - high.astype(F32)).astype(BF16)


def dot3(a_high, a_low, b_high, b_low):
    dot = functools.partial(jnp.dot, preferred_element_type=F32)
    return dot(a_high, b_high) + (dot(a_low, b_high) + dot(a_high, b_low))


def sum_kernel(
    ring, c_hbm, v_hbm, t_hbm, c_ref, near, scaled,
    acc, vt, got, t_ref, c_sem, l_sem,
    sib_send, sib_recv, y_send, y_recv, f_send, f_recv, r_send, r_recv, g_send, g_recv,
):
    row, col = lax.axis_index("row"), lax.axis_index("col")
    core, y = lax.rem(col, 2), lax.div(col, 2)
    sibling = y * 2 + (1 - core)
    across = (1 - y) * 2 + core
    across_sibling = (1 - y) * 2 + (1 - core)
    half = ring // 2
    z, x = lax.div(row, 2), lax.rem(row, 2)
    at = jnp.where(x == 0, z, ring - 1 - z)

    def row_of(place):
        return jnp.where(place < half, 2 * place, 2 * (ring - 1 - place) + 1)

    def wrap(i):
        return lax.rem(i + 2 * ring, ring)

    hops = (row_of(wrap(at + 1)), row_of(wrap(at - 1)))
    blocks, own, depth = near.shape
    width = c_ref.shape[2]
    part_depth = depth // HALVES
    steps = ring - 1

    def chunk_of(i):
        step = lax.div(i, 2) + 1
        return jnp.where(i == ring - 1, at, wrap(jnp.where(lax.rem(i, 2) == 0, at - step, at + step)))

    def c_copy(chunk):
        return pltpu.make_async_copy(
            c_hbm.at[:, pl.ds(pl.multiple_of(chunk * width, width), width)], c_ref.at[chunk], c_sem.at[chunk]
        )

    v_copy = pltpu.make_async_copy(v_hbm, near.at[col], l_sem.at[0])
    t_copy = pltpu.make_async_copy(t_hbm, t_ref, l_sem.at[1])
    v_copy.start()

    barrier = pltpu.get_barrier_semaphore()
    friends = [(row, sibling), (row, across), (hops[0], col), (hops[1], col)]
    for friend in friends:
        pl.semaphore_signal(barrier, inc=1, device_id=friend, device_id_type=MESH)
    pl.semaphore_wait(barrier, len(friends))

    def remote(src, dst, send, recv, to):
        return pltpu.make_async_remote_copy(
            src_ref=src, dst_ref=dst, send_sem=send, recv_sem=recv, device_id=to, device_id_type=MESH
        )

    size = own // PIECES

    def y_copy(h, q):
        there = (pl.ds(q * size, size), pl.ds(h * part_depth, part_depth))
        return remote(v_hbm.at[there], near.at[(col,) + there], y_send.at[h, q], y_recv.at[h, q], (row, across))

    def forward(h, q):
        there = (across, pl.ds(q * size, size), pl.ds(h * part_depth, part_depth))
        return remote(near.at[there], near.at[there], f_send.at[h, q], f_recv.at[h, q], (row, sibling))

    for h in range(HALVES):
        for q in range(PIECES):
            y_copy(h, q).start()
    sib = remote(v_hbm, near.at[col], sib_send, sib_recv, (row, sibling))
    sib.start()

    def load(i, carry):
        c_copy(chunk_of(i)).start()
        return carry

    lax.fori_loop(0, ring, load, 0)
    t_copy.start()

    def keep(block, h):
        high, low = split(near[block, :, h * part_depth:(h + 1) * part_depth].T)
        vt[h, block, :part_depth] = high
        vt[h, block, part_depth:] = low

    v_copy.wait()
    for h in range(HALVES):
        keep(col, h)
    sib.wait()
    for h in range(HALVES):
        keep(sibling, h)

    def arrive(h):
        for q in range(PIECES):
            y_copy(h, q).wait()
            forward(h, q).start()
        keep(across, h)
        for q in range(PIECES):
            forward(h, q).wait()
        keep(across_sibling, h)

    def job(i, h):
        chunk = chunk_of(i)
        total = None
        for b in range(blocks):
            high, low = split(c_ref[chunk, b * own:(b + 1) * own])
            both = jnp.dot(vt[h, b], high, preferred_element_type=F32)
            term = both[:part_depth] + (
                both[part_depth:] + jnp.dot(vt[h, b, :part_depth], low, preferred_element_type=F32)
            )
            total = term if total is None else total + term
        acc[chunk, h * part_depth:(h + 1) * part_depth] = total

    def first_job(i, carry):
        c_copy(chunk_of(i)).wait()
        job(i, 0)
        return carry

    def later_job(i, carry):
        job(i, 1)
        return carry

    part = part_depth // (2 * QUARTERS)

    def sum_send(h, way, step, q, src):
        rows = pl.ds(((h * 2 + way) * QUARTERS + q) * part, part)
        lane = h * 2 + way
        return remote(
            src.at[rows], got.at[step, rows], r_send.at[lane, step, q], r_recv.at[lane, step, q], (hops[way], col)
        )

    def begin(h):
        for q in range(QUARTERS):
            for way in range(2):
                sum_send(h, way, 0, q, acc.at[chunk_of(way)]).start()

    def reduce(h, step):
        for q in range(QUARTERS):
            for way in range(2):
                rows = pl.ds(((h * 2 + way) * QUARTERS + q) * part, part)
                chunk = wrap(at - 2 - step) if way == 0 else wrap(at + 2 + step)
                sum_send(h, way, step, q, got.at[step]).wait_recv()
                got[step, rows] += acc[chunk, rows]

                @pl.when(step < steps - 1)
                def _():
                    sum_send(h, way, step + 1, q, got.at[step]).start()

    arrive(0)
    lax.fori_loop(0, 2, first_job, 0)
    begin(0)
    lax.fori_loop(2, ring, first_job, 0)

    def early(t, carry):
        reduce(0, t)
        return carry

    def both_halves(t, carry):
        reduce(0, t)

        @pl.when(t >= LAG)
        def _():
            reduce(1, t - LAG)

        jobs = 2 * (t - LAG + 2)
        lax.fori_loop(jnp.minimum(jobs, ring), jnp.minimum(jobs + 2, ring), later_job, 0)
        return carry

    def late(t, carry):
        reduce(1, t - LAG)
        return carry

    lax.fori_loop(0, LAG - 1, early, 0)
    arrive(1)
    lax.fori_loop(0, 2, later_job, 0)
    begin(1)
    lax.fori_loop(LAG - 1, steps, both_halves, 0)
    t_copy.wait()
    t_high, t_low = split(t_ref[...])
    lax.fori_loop(steps, steps + LAG, late, 0)

    high, low = split(got[steps - 1])
    scaled[at] = dot3(t_high, t_low, high, low)
    g_part = depth // (2 * G_QUARTERS)

    def gather_send(way, step, q, chunk):
        ref = scaled.at[chunk, pl.ds((way * G_QUARTERS + q) * g_part, g_part)]
        return remote(ref, ref, g_send.at[way, step, q], g_recv.at[way, step, q], (hops[way], col))

    for q in range(G_QUARTERS):
        for way in range(2):
            gather_send(way, 0, q, at).start()

    def gather(step, carry):
        for q in range(G_QUARTERS):
            for way in range(2):
                chunk = wrap(at - 1 - step) if way == 0 else wrap(at + 1 + step)
                gather_send(way, step, q, chunk).wait_recv()

                @pl.when(step < steps - 1)
                def _():
                    gather_send(way, step + 1, q, chunk).start()

        return carry

    lax.fori_loop(0, steps, gather, 0)

    def sent(step, carry):
        for way in range(2):
            for h in range(HALVES):
                for q in range(QUARTERS):
                    sum_send(h, way, step, q, got.at[step]).wait_send()
            for q in range(G_QUARTERS):
                gather_send(way, step, q, at).wait_send()
        return carry

    lax.fori_loop(0, steps, sent, 0)


def update_kernel(c_ref, near, scaled, out_hbm, v_high, v_low, stage, sem):
    ring, height, width = c_ref.shape
    blocks, own, _ = near.shape
    for b in range(blocks):
        v_high[pl.ds(b * own, own)], v_low[pl.ds(b * own, own)] = split(near[b])
    slots = stage.shape[0]

    def out_copy(chunk, slot):
        return pltpu.make_async_copy(
            stage.at[slot], out_hbm.at[:, pl.ds(pl.multiple_of(chunk * width, width), width)], sem.at[slot]
        )

    def step(chunk, carry):
        slot = lax.rem(chunk, slots)

        @pl.when(chunk >= slots)
        def _():
            out_copy(chunk - slots, slot).wait()

        high, low = split(scaled[chunk])
        for b in range(blocks):
            rows = pl.ds(b * own, own)
            stage[slot, rows] = c_ref[chunk, rows] - dot3(v_high[rows], v_low[rows], high, low)
        out_copy(chunk, slot).start()
        return carry

    lax.fori_loop(0, ring, step, 0)
    for i in range(slots):
        chunk = ring - slots + i
        out_copy(chunk, chunk % slots).wait()


def ring_shards(ring, trailing, vectors, tfactor):
    height, columns = trailing.shape
    own, depth = vectors.shape
    width = columns // ring
    blocks = height // own
    steps = ring - 1
    dma = pltpu.SemaphoreType.DMA
    vmem = pl.BlockSpec(memory_space=pltpu.VMEM)
    hbm = pl.BlockSpec(memory_space=pl.ANY)
    held, near, scaled = pl.pallas_call(
        functools.partial(sum_kernel, ring),
        out_shape=(
            pltpu.VMEM((ring, height, width), F32),
            pltpu.VMEM((blocks, own, depth), F32),
            pltpu.VMEM((ring, depth, width), F32),
        ),
        in_specs=[hbm, hbm, hbm],
        out_specs=(vmem, vmem, vmem),
        scratch_shapes=[
            pltpu.VMEM((ring, depth, width), F32),
            pltpu.VMEM((HALVES, blocks, 2 * depth // HALVES, own), BF16),
            pltpu.VMEM((steps, depth, width), F32),
            pltpu.VMEM((depth, depth), F32),
            dma((ring,)), dma((2,)),
            dma, dma,
            dma((HALVES, PIECES)), dma((HALVES, PIECES)), dma((HALVES, PIECES)), dma((HALVES, PIECES)),
            dma((2 * HALVES, steps, QUARTERS)), dma((2 * HALVES, steps, QUARTERS)),
            dma((2, steps, G_QUARTERS)), dma((2, steps, G_QUARTERS)),
        ],
        compiler_params=pltpu.CompilerParams(
            collective_id=0, has_side_effects=True, vmem_limit_bytes=20 << 20
        ),
    )(trailing, vectors, tfactor)
    slots = min(4, ring)
    return pl.pallas_call(
        update_kernel,
        out_shape=jax.ShapeDtypeStruct((height, columns), F32),
        in_specs=[vmem, vmem, vmem],
        out_specs=hbm,
        scratch_shapes=[
            pltpu.VMEM((height, depth), BF16),
            pltpu.VMEM((height, depth), BF16),
            pltpu.VMEM((slots, height, width), F32),
            dma((slots,)),
        ],
        compiler_params=pltpu.CompilerParams(vmem_limit_bytes=20 << 20),
    )(held, near, scaled)


def plain_shards(trailing, vectors, tfactor):
    dot = functools.partial(jnp.dot, precision=lax.Precision.HIGH, preferred_element_type=F32)
    near_vectors = lax.all_gather(vectors, "col", axis=0, tiled=True)
    summed = lax.psum(dot(near_vectors.T, trailing), "row")
    return trailing - dot(near_vectors, dot(tfactor, summed))


def solution(mesh):
    ring, columns = mesh.shape["row"], mesh.shape["col"]
    placed = (P("row", "col"), P(("row", "col"), None), P())

    def shards(trailing, vectors, tfactor):
        width = trailing.shape[1] // ring
        if columns == 4 and ring % 2 == 0 and ring > 2 * LAG and width % 128 == 0:
            return ring_shards(ring, trailing, vectors, tfactor)
        return plain_shards(trailing, vectors, tfactor)

    return jax.shard_map(
        shards, mesh=mesh, in_specs=placed, out_specs=P("row", "col"), check_vma=False
    )
```

time: 88.6 us -> 89.2 us (level)
  no operation moved by 1% of the time
where the time goes in v2:
time: 89.2 us; the launch traced here: 89 us
  Pallas kernels  87 us (98%)
  local copies, waits for them, and re-layouts  1.99 us (2%)
    pallas_call x1, Pallas kernels, ring_shards(): pl.pallas_call(functools.partial(sum_kernel, ring), out_shape=(pltpu.VMEM...  77.4 us
    pallas_call x1, Pallas kernels, ring_shards(): pl.pallas_call(update_kernel, out_shape=jax.ShapeDtypeStruct((height, col...  9.63 us
    unnamed x4, local copies, waits for them, and re-layouts  1.99 us

profile of v2, /device:TPU:0, one launch (start us, length us, event | category | flops | bytes accessed | tf_op | source)
XLA Modules:
  0.0 89.0 jit_solution(9176654794169150393)
XLA Ops:
  0.0 0.0 copy-start
  0.0 1.0 %copy-done = f32[512,256]{1,0:T(8,128)S(1)} copy-done((f32[512,256]{1,0:T(8,128)S(1)}, f32[512,256]{1,0:T(8,128)}, u32[]{:S(2)}) %copy-start) | copy-done | bytes 524312
  1.0 0.0 copy-start.1
  1.0 0.9 %copy-done.1 = f32[256,256]{1,0:T(8,128)S(1)} copy-done((f32[256,256]{1,0:T(8,128)S(1)}, f32[256,256]{1,0:T(8,128)}, u32[]{:S(2)}) %copy-start.1) | copy-done | bytes 262168
  2.0 77.4 %shard_map.37 = (f32[8,2048,256]{2,1,0:T(8,128)S(1)}, f32[4,512,256]{2,1,0:T(8,128)S(1)}, f32[8,256,256]{2,1,0:T(8,128)S(1)}) custom-call(f32[2048,2048]{1,0:T(8,128)} %c_hbm.1, f32[512,256]{1,0:T(8,128)S(1)} %copy-done, f32[256,256]{1,0:T(8,128)S(1)} %copy-done.1), custom_call_target="tpu_custom_call" | custom-call | tf_op jit(solution)/shard_map/pallas_call | solution.py:282
  79.4 9.6 %shard_map.38 = f32[2048,2048]{1,0:T(8,128)} custom-call(f32[8,2048,256]{2,1,0:T(8,128)S(1)} %get-tuple-element.8.c_ref, f32[4,512,256]{2,1,0:T(8,128)S(1)} %get-tuple-element.9.near, f32[8,256,256]{2,1,0:T(8,128)S(1)} %get-tuple-element.10.scaled), custom_call_target="tpu_custom_call" | custom-call | tf_op jit(solution)/shard_map/pallas_call | solution.py:307
Async XLA Ops:
  0.0 1.0 %copy-start = (f32[512,256]{1,0:T(8,128)S(1)}, f32[512,256]{1,0:T(8,128)}, u32[]{:S(2)}) copy-start(f32[512,256]{1,0:T(8,128)} %v_hbm.1) | copy-start | bytes 1572868
  1.0 0.9 %copy-start.1 = (f32[256,256]{1,0:T(8,128)S(1)}, f32[256,256]{1,0:T(8,128)}, u32[]{:S(2)}) copy-start(f32[256,256]{1,0:T(8,128)} %t_hbm.1) | copy-start | bytes 786436

commit v3 on v2

--- a/solution.py
+++ b/solution.py
@@ -13,7 +13,7 @@
 PIECES = 2
 QUARTERS = 2
 G_QUARTERS = 4
-LAG = 3
+LAG = 2
 
 
 def split(x):
@@ -80,16 +80,17 @@
 
     def y_copy(h, q):
         there = (pl.ds(q * size, size), pl.ds(h * part_depth, part_depth))
-        return remote(v_hbm.at[there], near.at[(col,) + there], y_send.at[h, q], y_recv.at[h, q], (row, across))
+        return remote(near.at[(col,) + there], near.at[(col,) + there], y_send.at[h, q], y_recv.at[h, q], (row, across))
 
     def forward(h, q):
         there = (across, pl.ds(q * size, size), pl.ds(h * part_depth, part_depth))
         return remote(near.at[there], near.at[there], f_send.at[h, q], f_recv.at[h, q], (row, sibling))
 
+    v_copy.wait()
     for h in range(HALVES):
         for q in range(PIECES):
             y_copy(h, q).start()
-    sib = remote(v_hbm, near.at[col], sib_send, sib_recv, (row, sibling))
+    sib = remote(near.at[col], near.at[col], sib_send, sib_recv, (row, sibling))
     sib.start()
 
     def load(i, carry):
@@ -104,7 +105,6 @@
         vt[h, block, :part_depth] = high
         vt[h, block, part_depth:] = low
 
-    v_copy.wait()
     for h in range(HALVES):
         keep(col, h)
     sib.wait()
@@ -120,20 +120,29 @@
             forward(h, q).wait()
         keep(across_sibling, h)
 
+    def product(h, block, high, low):
+        both = jnp.dot(vt[h, block], high, preferred_element_type=F32)
+        return both[:part_depth] + (
+            both[part_depth:] + jnp.dot(vt[h, block, :part_depth], low, preferred_element_type=F32)
+        )
+
+    def pieces_of(chunk, pair):
+        return [(b, split(c_ref[chunk, pl.ds(pl.multiple_of(b * own, own), own)])) for b in pair]
+
+    def near_job(i, carry):
+        chunk = chunk_of(i)
+        c_copy(chunk).wait()
+        (b0, c0), (b1, c1) = pieces_of(chunk, (col, sibling))
+        for h in range(HALVES):
+            acc[chunk, h * part_depth:(h + 1) * part_depth] = product(h, b0, *c0) + product(h, b1, *c1)
+        return carry
+
     def job(i, h):
         chunk = chunk_of(i)
-        total = None
-        for b in range(blocks):
-            high, low = split(c_ref[chunk, b * own:(b + 1) * own])
-            both = jnp.dot(vt[h, b], high, preferred_element_type=F32)
-            term = both[:part_depth] + (
-                both[part_depth:] + jnp.dot(vt[h, b, :part_depth], low, preferred_element_type=F32)
-            )
-            total = term if total is None else total + term
-        acc[chunk, h * part_depth:(h + 1) * part_depth] = total
+        (b0, c0), (b1, c1) = pieces_of(chunk, (across, across_sibling))
+        acc[chunk, h * part_depth:(h + 1) * part_depth] += product(h, b0, *c0) + product(h, b1, *c1)
 
     def first_job(i, carry):
-        c_copy(chunk_of(i)).wait()
         job(i, 0)
         return carry
 
@@ -167,6 +176,7 @@
                 def _():
                     sum_send(h, way, step + 1, q, got.at[step]).start()
 
+    lax.fori_loop(0, ring, near_job, 0)
     arrive(0)
     lax.fori_loop(0, 2, first_job, 0)
     begin(0)

time: 89.2 us -> 85.1 us (0.954)
  Pallas kernels: 87 us -> 82.9 us
    pallas_call x1, Pallas kernels: 77.4 us -> 73.3 us  [ring_shards(): pl.pallas_call(functools.partial(sum_kernel, ring), out_shape=(pltpu.VMEM...]
where the time goes in v3:
time: 85.1 us; the launch traced here: 84.9 us
  Pallas kernels  82.9 us (97%)
  local copies, waits for them, and re-layouts  1.99 us (2%)
    pallas_call x1, Pallas kernels, ring_shards(): pl.pallas_call(functools.partial(sum_kernel, ring), out_shape=(pltpu.VMEM...  73.3 us
    pallas_call x1, Pallas kernels, ring_shards(): pl.pallas_call(update_kernel, out_shape=jax.ShapeDtypeStruct((height, col...  9.63 us
    unnamed x4, local copies, waits for them, and re-layouts  1.99 us

profile of v3, /device:TPU:0, one launch (start us, length us, event | category | flops | bytes accessed | tf_op | source)
XLA Modules:
  0.0 84.9 jit_solution(14459187385965756867)
XLA Ops:
  0.0 0.0 copy-start
  0.0 1.0 %copy-done = f32[512,256]{1,0:T(8,128)S(1)} copy-done((f32[512,256]{1,0:T(8,128)S(1)}, f32[512,256]{1,0:T(8,128)}, u32[]{:S(2)}) %copy-start) | copy-done | bytes 524312
  1.0 0.0 copy-start.1
  1.0 0.9 %copy-done.1 = f32[256,256]{1,0:T(8,128)S(1)} copy-done((f32[256,256]{1,0:T(8,128)S(1)}, f32[256,256]{1,0:T(8,128)}, u32[]{:S(2)}) %copy-start.1) | copy-done | bytes 262168
  2.0 73.3 %shard_map.37 = (f32[8,2048,256]{2,1,0:T(8,128)S(1)}, f32[4,512,256]{2,1,0:T(8,128)S(1)}, f32[8,256,256]{2,1,0:T(8,128)S(1)}) custom-call(f32[2048,2048]{1,0:T(8,128)} %c_hbm.1, f32[512,256]{1,0:T(8,128)S(1)} %copy-done, f32[256,256]{1,0:T(8,128)S(1)} %copy-done.1), custom_call_target="tpu_custom_call" | custom-call | tf_op jit(solution)/shard_map/pallas_call | solution.py:292
  75.3 9.6 %shard_map.38 = f32[2048,2048]{1,0:T(8,128)} custom-call(f32[8,2048,256]{2,1,0:T(8,128)S(1)} %get-tuple-element.8.c_ref, f32[4,512,256]{2,1,0:T(8,128)S(1)} %get-tuple-element.9.near, f32[8,256,256]{2,1,0:T(8,128)S(1)} %get-tuple-element.10.scaled), custom_call_target="tpu_custom_call" | custom-call | tf_op jit(solution)/shard_map/pallas_call | solution.py:317
Async XLA Ops:
  0.0 1.0 %copy-start = (f32[512,256]{1,0:T(8,128)S(1)}, f32[512,256]{1,0:T(8,128)}, u32[]{:S(2)}) copy-start(f32[512,256]{1,0:T(8,128)} %v_hbm.1) | copy-start | bytes 1572868
  1.0 0.9 %copy-start.1 = (f32[256,256]{1,0:T(8,128)S(1)}, f32[256,256]{1,0:T(8,128)}, u32[]{:S(2)}) copy-start(f32[256,256]{1,0:T(8,128)} %t_hbm.1) | copy-start | bytes 786436

commit v4 on v3

--- a/solution.py
+++ b/solution.py
@@ -10,9 +10,9 @@
 MESH = pl.DeviceIdType.MESH
 F32, BF16 = jnp.float32, jnp.bfloat16
 HALVES = 2
-PIECES = 2
+PIECES = 4
 QUARTERS = 2
-G_QUARTERS = 4
+G_QUARTERS = 8
 LAG = 2
 
 

time: 85.1 us -> 84.7 us (level)
  no operation moved by 1% of the time
where the time goes in v4:
time: 84.7 us; the launch traced here: 84.5 us
  Pallas kernels  82.5 us (97%)
  local copies, waits for them, and re-layouts  1.99 us (2%)
    pallas_call x1, Pallas kernels, ring_shards(): pl.pallas_call(functools.partial(sum_kernel, ring), out_shape=(pltpu.VMEM...  72.9 us
    pallas_call x1, Pallas kernels, ring_shards(): pl.pallas_call(update_kernel, out_shape=jax.ShapeDtypeStruct((height, col...  9.63 us
    unnamed x4, local copies, waits for them, and re-layouts  1.99 us

profile of v4, /device:TPU:0, one launch (start us, length us, event | category | flops | bytes accessed | tf_op | source)
XLA Modules:
  0.0 84.5 jit_solution(4501055088334460474)
XLA Ops:
  0.0 0.0 copy-start
  0.0 1.0 %copy-done = f32[512,256]{1,0:T(8,128)S(1)} copy-done((f32[512,256]{1,0:T(8,128)S(1)}, f32[512,256]{1,0:T(8,128)}, u32[]{:S(2)}) %copy-start) | copy-done | bytes 524312
  1.0 0.0 copy-start.1
  1.0 0.9 %copy-done.1 = f32[256,256]{1,0:T(8,128)S(1)} copy-done((f32[256,256]{1,0:T(8,128)S(1)}, f32[256,256]{1,0:T(8,128)}, u32[]{:S(2)}) %copy-start.1) | copy-done | bytes 262168
  2.0 72.9 %shard_map.37 = (f32[8,2048,256]{2,1,0:T(8,128)S(1)}, f32[4,512,256]{2,1,0:T(8,128)S(1)}, f32[8,256,256]{2,1,0:T(8,128)S(1)}) custom-call(f32[2048,2048]{1,0:T(8,128)} %c_hbm.1, f32[512,256]{1,0:T(8,128)S(1)} %copy-done, f32[256,256]{1,0:T(8,128)S(1)} %copy-done.1), custom_call_target="tpu_custom_call" | custom-call | tf_op jit(solution)/shard_map/pallas_call | solution.py:292
  74.9 9.6 %shard_map.38 = f32[2048,2048]{1,0:T(8,128)} custom-call(f32[8,2048,256]{2,1,0:T(8,128)S(1)} %get-tuple-element.8.c_ref, f32[4,512,256]{2,1,0:T(8,128)S(1)} %get-tuple-element.9.near, f32[8,256,256]{2,1,0:T(8,128)S(1)} %get-tuple-element.10.scaled), custom_call_target="tpu_custom_call" | custom-call | tf_op jit(solution)/shard_map/pallas_call | solution.py:317
Async XLA Ops:
  0.0 1.0 %copy-start = (f32[512,256]{1,0:T(8,128)S(1)}, f32[512,256]{1,0:T(8,128)}, u32[]{:S(2)}) copy-start(f32[512,256]{1,0:T(8,128)} %v_hbm.1) | copy-start | bytes 1572868
  1.0 0.9 %copy-start.1 = (f32[256,256]{1,0:T(8,128)S(1)}, f32[256,256]{1,0:T(8,128)}, u32[]{:S(2)}) copy-start(f32[256,256]{1,0:T(8,128)} %t_hbm.1) | copy-start | bytes 786436
